TPU v7x, 256 devices: a whole 4x4x8 slice. The times are simulated.
256 devices in a mesh: tp: 16 (over z_lo, y), dp: 16 (over z_hi, x, core).
Axes of the slice: x: 4, y: 4, z: 8 (z_hi: 2, z_lo: 4; z = z_hi * 4 + z_lo), core: 2. Of those that a mesh axis runs over, the one named last changes fastest.
Arguments:
- normed: bfloat16 [8192, 4096], P(('dp', 'tp')), may hold values from -6 to 6
- cotangent: bfloat16 [8192, 8192], P('dp', 'tp'), may hold values from -0.52734375 to 0.52734375
- weight_tiles: bfloat16 [2, 2048, 128, 128], P(None, 'tp'), may hold values from -0.09375 to 0.09375
- slot_tile: int32 [2048], replicated, may hold values from 0 to 2047, as said below
Outputs:
- hidden: bfloat16 [8192, 8192], P('dp', 'tp')
- d_normed: bfloat16 [8192, 4096], P(('dp', 'tp'))
- grad_tiles: float32 [2, 2048, 128, 128], P(None, 'tp', 'dp')
Inputs may be any that keep to these rules, and one draw needn't show every extreme that they name: `slot_tile`: A permutation of 0 to 2047. Position p belongs to owner p // 128 at slot p % 128. Each owner holds 6 to 10 tiles of the tile columns t * 4 to (t + 1) * 4 - 1 of each index t of tp; in every draw some owner holds exactly 10 for some t.
All inputs are finite; a program needn't handle non-finite values.
Results may differ from a plain program's by a relative error of at most 0.018.
Values may be sent and summed in bfloat16 or wider, within the bound.
A program may use at most 128 MiB of HBM per device.

v0:
```python
import jax
import jax.numpy as jnp
from jax import lax
from jax.sharding import Mesh
from jax.sharding import PartitionSpec as P

D = 4096
FW = 8192
TILE = 128
TP = ("tp_0", "tp_1")
DP_TP = ("dp", "tp_0", "tp_1")


def joined_along(tiles, dim):
    dims = list(tiles.shape[1:])
    dims[dim] *= tiles.shape[0]
    return jnp.moveaxis(tiles, 0, dim).reshape(dims)


def all_blocks(array, axes, order):
    tiles = array
    for k in order:
        tiles = lax.all_gather(tiles, axes[k])
    done = order[::-1]
    back = [done.index(k) for k in range(len(axes))]
    tiles = tiles.transpose(*back, *range(len(axes), tiles.ndim))
    return tiles.reshape(-1, *array.shape)


def whole_of(array, axes, order, dim):
    return joined_along(all_blocks(array, axes, order), dim)


def own_block(tiles, axes, order):
    inside = tiles.shape[1:]
    tiles = tiles.reshape(*(lax.axis_size(a) for a in axes), *inside)
    tiles = jnp.moveaxis(tiles, order, range(len(axes))).reshape(-1, *inside)
    for k in order:
        tiles = lax.psum_scatter(tiles, axes[k], scatter_dimension=0, tiled=True)
    return tiles[0]


def cut_along(array, dim, count):
    before, after = (array.shape[:dim], array.shape[dim + 1 :])
    return jnp.moveaxis(array.reshape(*before, count, -1, *after), dim, 0)


def sum_by_axis(array, axes, order, dim):
    count = lax.axis_size(axes)
    return own_block(cut_along(array, dim, count), axes, order)


def build_lists(slot_tile, groups, owned_count, tile_cols, cols_dev, list_len):
    owned_tiles = slot_tile.reshape(groups, owned_count)
    target = owned_tiles % tile_cols // cols_dev
    matches = (target[:, :, None] == jnp.arange(groups, dtype=jnp.int32)[None, None, :]).astype(
        jnp.int32
    )
    running = jnp.cumsum(matches, axis=1) - 1
    rank_of = jnp.sum(running * matches, axis=2)
    owner_ix = jnp.broadcast_to(jnp.arange(groups, dtype=jnp.int32)[:, None], (groups, owned_count))
    slot_ix = jnp.broadcast_to(
        jnp.arange(owned_count, dtype=jnp.int32)[None, :], (groups, owned_count)
    )
    table = jnp.full((groups, groups, list_len), -1, jnp.int32)
    return table.at[owner_ix, target, rank_of].set(slot_ix, mode="drop")


def incoming_places(in_lists, slot_tile, consumer, tile_cols, cols_dev, owned_count):
    groups = in_lists.shape[0]
    present = in_lists >= 0
    position = jnp.arange(groups, dtype=jnp.int32)[:, None] * owned_count + jnp.maximum(in_lists, 0)
    tile_id = slot_tile[position]
    tile_row = tile_id // tile_cols
    tile_col = tile_id % tile_cols - consumer * cols_dev
    local_idx = tile_row * cols_dev + tile_col
    return (jnp.where(present, local_idx, owned_count), present)


def pick_tiles(source, indices, present):
    limit = source.shape[1] - 1
    picked = source[:, jnp.minimum(indices, limit)]
    mask = present.reshape((1,) + present.shape + (1,) * (source.ndim - 2))
    return jnp.where(mask, picked, jnp.zeros((), source.dtype))


def place_tiles(arrived, places, owned_count):
    flat = arrived.reshape((arrived.shape[0], -1) + arrived.shape[3:])
    empty = jnp.zeros((arrived.shape[0], owned_count) + arrived.shape[3:], arrived.dtype)
    return empty.at[:, places.reshape(-1)].set(flat, mode="drop")


def local(normed, cotangent, weight_tiles, slot_tile):
    tp_size = lax.axis_size(TP)
    consumer = lax.axis_index(TP)
    owned_count = weight_tiles.shape[1]
    tile_size = weight_tiles.shape[2]
    tile_rows = D // TILE
    tile_cols = FW // TILE
    cols_dev = tile_cols // tp_size
    base_count = owned_count // tp_size
    list_len = base_count + base_count // 4
    send_lists = build_lists(slot_tile, tp_size, owned_count, tile_cols, cols_dev, list_len)
    my_lists = lax.dynamic_index_in_dim(send_lists, consumer, 0, keepdims=False)
    out_present = my_lists >= 0
    out_places = jnp.where(out_present, my_lists, owned_count)
    in_lists = lax.dynamic_index_in_dim(send_lists, consumer, 1, keepdims=False)
    in_places, in_present = incoming_places(
        in_lists, slot_tile, consumer, tile_cols, cols_dev, owned_count
    )
    slab_rows = tile_size // lax.axis_size("dp")
    slab_start = lax.axis_index("dp") * slab_rows
    own_rows = lax.dynamic_slice_in_dim(weight_tiles, slab_start, slab_rows, 2)
    outgoing = pick_tiles(own_rows, my_lists, out_present)
    arrived = lax.all_to_all(outgoing, TP, split_axis=1, concat_axis=1, tiled=True)
    partial_tiles = place_tiles(arrived, in_places, owned_count)
    weight_block = lax.all_gather(partial_tiles, "dp", axis=2, tiled=True)
    weight_block = weight_block.reshape(2, tile_rows, cols_dev, tile_size, tile_size)
    gathered = whole_of(normed, TP, (0, 1), 0)
    group_rows = gathered.shape[0]
    tiled_in = gathered.reshape(group_rows, tile_rows, tile_size)
    both_proj = jnp.einsum(
        "nri,mrcij->nmcj", tiled_in, weight_block, preferred_element_type=jnp.float32
    )
    gate_proj = both_proj[:, 0].reshape(group_rows, -1)
    up_proj = both_proj[:, 1].reshape(group_rows, -1)
    sigmoid_gate = jax.nn.sigmoid(gate_proj)
    act_gate = gate_proj * sigmoid_gate
    hidden = (act_gate * up_proj).astype(jnp.bfloat16)
    cot_full = cotangent.astype(jnp.float32)
    grad_gate = (
        cot_full * up_proj * (sigmoid_gate * (1.0 + gate_proj * (1.0 - sigmoid_gate)))
    ).astype(jnp.bfloat16)
    grad_up = (cot_full * act_gate).astype(jnp.bfloat16)
    grads_in = jnp.stack([grad_gate, grad_up], 1).reshape(group_rows, 2, cols_dev, tile_size)
    term = jnp.einsum("nmcj,mrcij->nri", grads_in, weight_block, preferred_element_type=jnp.float32)
    d_normed = (
        sum_by_axis(
            term.reshape(normed.shape[0] * lax.axis_size(TP), -1).astype(jnp.bfloat16),
            TP,
            (1, 0),
            0,
        )
        .astype(jnp.float32)
        .astype(jnp.bfloat16)
    )
    partial_value = jnp.einsum(
        "nri,nmcj->mrcij", tiled_in, grads_in, preferred_element_type=jnp.float32
    ).astype(jnp.bfloat16)
    partial_value = partial_value.reshape(2, owned_count, tile_size, tile_size)
    summed = lax.psum_scatter(partial_value, "dp", scatter_dimension=2, tiled=True).astype(
        jnp.float32
    )
    outgoing_grads = pick_tiles(summed, in_places, in_present)
    returned = lax.all_to_all(
        outgoing_grads.astype(jnp.bfloat16), TP, split_axis=1, concat_axis=1, tiled=True
    ).astype(outgoing_grads.dtype)
    result = place_tiles(returned, out_places, owned_count)
    return (hidden, d_normed, result)


def solution(mesh):
    finer = Mesh(mesh.devices.reshape(4, 4, mesh.shape["dp"]), ("tp_0", "tp_1", "dp"))
    placed = (P(DP_TP, None), P("dp", TP), P(None, TP, None, None), P())
    return jax.shard_map(
        local,
        mesh=finer,
        in_specs=placed,
        out_specs=(P("dp", TP), P(DP_TP, None), P(None, TP, "dp", None)),
        check_vma=False,
    )
```

profile of v0, /device:TPU:64, one launch (start us, length us, event | category | flops | bytes accessed | tf_op | source)
XLA Modules:
  0.0 496.8 jit_solution(926852536485832651)
XLA Ops:
  7.2 0.7 all-gather.8.cloned.1.call-update
  8.0 36.1 %all-gather.8.cloned.1.call-done = bf16[128,4096]{1,0:T(8,128)(2,1)} async-done(((bf16[32,4096]{1,0:T(8,128)(2,1)}), bf16[128,4096]{1,0:T(8,128)(2,1)}) %all-gather.8.cloned.1.call-update) | async-done | bytes 1048592 | tf_op jit(solution)/shard_map/all_gather | solution.py:23
  44.0 0.7 add_select_fusion
  44.8 0.1 copy.92
  44.9 2.8 select_reduce_fusion
  47.7 0.7 compare_select_fusion.3
  48.5 0.7 multiply_reduce_fusion
  49.2 0.7 and_reduce_fusion
  49.9 8.1 %scatter_custom_fusion.2 = s32[2560]{0:T(1024)S(1)} fusion(s32[2048]{0:T(1024)S(1)} %select_bitcast_fusion.1, s32[2048]{0:T(1024)S(1)} %iota_bitcast_fusion, s32[]{:T(128)} %constant.88.clone.1), kind=kCustom, calls=%fused_computation.81 | custom fusion | bytes 10244
  58.0 0.1 reshape.536
  58.1 0.1 copy.97
  58.2 0.1 reshape.550
  58.3 0.1 copy.96
  58.4 1.1 constant_dynamic-slice_fusion
  59.6 0.8 gather_fusion.1
  60.4 1.1 select_bitcast_fusion
  61.5 6.7 %all-to-all-start = ((bf16[2,16,10,8,128]{4,3,0,2,1:T(8,128)(2,1)}), bf16[2,16,10,8,128]{4,3,0,2,1:T(8,128)(2,1)S(1)}, u32[]{:S(2)}, u32[]{:S(2)}) async-start(bf16[2,16,10,8,128]{4,3,0,2,1:T(8,128)(2,1)} %select_bitcast_fusion), calls=%async_computation | async-start | bytes 1310720 | tf_op jit(solution)/shard_map/all_to_all | solution.py:115
  68.2 0.1 compare_bitcast_fusion
  68.3 0.2 copy.94
  68.5 0.1 ge.52
  68.6 0.3 bitcast_reduce_fusion
  68.9 0.1 copy.95
  69.0 0.1 reshape.542
  69.1 1.4 gather_fusion
  70.6 14.5 %all-to-all-done = bf16[2,16,10,8,128]{4,3,0,2,1:T(8,128)(2,1)S(1)} async-done(((bf16[2,16,10,8,128]{4,3,0,2,1:T(8,128)(2,1)}), bf16[2,16,10,8,128]{4,3,0,2,1:T(8,128)(2,1)S(1)}, u32[]{:S(2)}, u32[]{:S(2)}) %all-to-all-start) | async-done | bytes 655392 | tf_op jit(solution)/shard_map/all_to_all | solution.py:115
  85.2 6.9 %scatter_fusion = bf16[2,128,8,128]{3,2,1,0:T(8,128)(2,1)S(1)} fusion(bf16[2,128,8,128]{3,2,1,0:T(8,128)(2,1)S(1)} %broadcast_in_dim.63, s32[160]{0:T(256)S(1)} %bitcast.163, bf16[160,2,8,128]{3,2,1,0:T(8,128)(2,1)S(1)} %bitcast.151), kind=kCustom, calls=%fused_computation.3 | custom fusion | bytes 1966720 | tf_op jit(solution)/shard_map/scatter | solution.py:90
  92.0 0.8 copy-done.1
  92.9 0.2 reduce-scatter.6.cloned.1.call-start
  93.1 0.2 copy.101
  93.3 10.9 %all-gather.10.cloned.1.call-done = bf16[16,32,4096]{2,1,0:T(8,128)(2,1)} async-done(((bf16[4,32,4096]{2,1,0:T(8,128)(2,1)}), bf16[16,32,4096]{2,1,0:T(8,128)(2,1)}) %all-gather.10.cloned.1.call-update) | async-done | bytes 4194320 | tf_op jit(solution)/shard_map/all_gather | solution.py:23
  104.2 2.5 copy.98
  106.6 3.2 copy.134
  109.9 108.0 %all-gather.6.cloned.1.call-done = bf16[2,128,128,128]{3,2,1,0:T(8,128)(2,1)} async-done(((bf16[2,128,8,128]{3,2,1,0:T(8,128)(2,1)}), bf16[2,128,128,128]{3,2,1,0:T(8,128)(2,1)}) %all-gather.6.cloned.1.call-update) | async-done | bytes 8388624 | tf_op jit(solution)/shard_map/all_gather | solution.py:117
  217.9 10.5 %fusion.4 = f32[512,2,4,128]{0,3,2,1:T(8,128)S(1)} fusion(bf16[2,32,4,128,128]{4,3,2,1,0:T(8,128)(2,1)} %bitcast.144, bf16[512,32,128,1,1]{2,1,0,4,3:T(8,128)(2,1)} %bitcast.148), kind=kOutput, calls=%fused_computation.13 | convolution fusion | flops 4294967296 | bytes 14680064 | tf_op jit(solution)/shard_map/nri,mrcij->nmcj/dot_general | solution.py:122
  228.4 0.2 fusion.37
  228.6 10.3 %copy.104 = bf16[32,128,4,128,2]{3,1,0,4,2:T(8,128)(2,1)} copy(bf16[32,128,4,128,2]{3,1,2,0,4:T(8,128)(2,1)} %bitcast.145) | data formatting | bytes 16777216 | tf_op jit(solution)/shard_map/nmcj,mrcij->nri/dot_general | solution.py:136
  238.9 0.7 fusion.8
  239.6 0.3 copy.103
  239.9 0.3 copy.102
  240.2 8.2 %bitcast_convert_fusion = bf16[512,4096]{1,0:T(8,128)(2,1)S(1)} fusion(bf16[4096,4,128,2]{2,0,3,1:T(8,128)(2,1)} %bitcast.146, bf16[512,1,4,128]{3,0,1,2:T(8,128)(2,1)S(1)} %copy.103, bf16[512,1,4,128]{3,0,1,2:T(8,128)(2,1)S(1)} %copy.102), kind=kOutput, calls=%fused_computation.7 | convolution fusion | flops 4297588736 | bytes 13631488 | tf_op jit(solution)/shard_map/nmcj,mrcij->nri/dot_general | solution.py:136
  248.3 2.5 copy.105
  250.9 9.6 %convert_bitcast_fusion = bf16[2,32,4,128,128]{3,4,1,2,0:T(8,128)(2,1)} fusion(bf16[512,32,128,1,1]{2,1,0,4,3:T(8,128)(2,1)} %bitcast.149, bf16[512,1,4,128]{3,0,1,2:T(8,128)(2,1)S(1)} %copy.103, bf16[512,1,4,128]{3,0,1,2:T(8,128)(2,1)S(1)} %copy.102), kind=kOutput, calls=%fused_computation.8 | convolution fusion | flops 4299685888 | bytes 13631488 | tf_op jit(solution)/shard_map/nri,nmcj->mrcij/dot_general | solution.py:147
  260.5 12.1 %copy.110 = bf16[2,32,4,128,128]{4,3,2,1,0:T(8,128)(2,1)} copy(bf16[2,32,4,128,128]{3,4,1,2,0:T(8,128)(2,1)} %convert_bitcast_fusion) | data formatting | bytes 16777216 | tf_op jit(solution)/shard_map/convert_element_type | solution.py:149
  272.6 12.1 %copy.132 = bf16[2,128,128,128]{3,1,0,2:T(8,128)(2,1)} copy(bf16[2,128,128,128]{3,2,1,0:T(8,128)(2,1)} %bitcast.140) | data formatting | bytes 16777216
  284.7 13.9 %copy.150 = bf16[16,8,256,128]{3,1,2,0:T(8,128)(2,1)} copy(bf16[16,8,256,128]{3,2,1,0:T(8,128)(2,1)} %bitcast.141) | data formatting | bytes 16777216
  298.7 0.1 gather.16
  298.8 0.1 copy.116
  298.9 0.1 copy.112
  298.9 0.2 reduce-scatter.8.cloned.1.call-update
  299.3 0.1 copy.117
  299.3 0.1 reshape.558
  299.5 141.2 %reduce-scatter.10.cloned.1.call-done = bf16[8,32768]{1,0:T(8,128)(2,1)} async-done(((bf16[128,32768]{1,0:T(8,128)(2,1)}), bf16[8,32768]{1,0:T(8,128)(2,1)}) %reduce-scatter.10.cloned.1.call-update) | async-done | bytes 524304
  440.7 1.1 copy.136
  441.8 0.3 copy.149
  442.1 0.8 gather_fusion.2
  442.9 1.1 fusion.20
  444.0 6.8 %all-to-all-start.1 = ((bf16[2,16,10,8,128]{4,3,0,2,1:T(8,128)(2,1)}), bf16[2,16,10,8,128]{4,3,0,2,1:T(8,128)(2,1)S(1)}, u32[]{:S(2)}, u32[]{:S(2)}) async-start(bf16[2,16,10,8,128]{4,3,0,2,1:T(8,128)(2,1)} %fusion.20), calls=%async_computation.3 | async-start | bytes 1310720 | tf_op jit(solution)/shard_map/all_to_all | solution.py:155
  450.8 0.1 copy.106
  450.9 0.1 squeeze.10
  451.0 1.0 copy.118
  452.0 30.0 %all-to-all-done.1 = bf16[2,16,10,8,128]{4,3,0,2,1:T(8,128)(2,1)S(1)} async-done(((bf16[2,16,10,8,128]{4,3,0,2,1:T(8,128)(2,1)}), bf16[2,16,10,8,128]{4,3,0,2,1:T(8,128)(2,1)S(1)}, u32[]{:S(2)}, u32[]{:S(2)}) %all-to-all-start.1) | async-done | bytes 655392 | tf_op jit(solution)/shard_map/all_to_all | solution.py:155
  482.0 0.1 convert_bitcast_fusion.1
  482.2 6.8 %scatter_fusion.1 = f32[2,128,8,128]{3,2,1,0:T(8,128)S(1)} fusion(f32[2,128,8,128]{3,2,1,0:T(8,128)S(1)} %broadcast_in_dim.71, s32[160]{0:T(256)S(1)} %bitcast.164, f32[160,2,8,128]{3,2,1,0:T(8,128)S(1)} %convert_bitcast_fusion.1), kind=kCustom, calls=%fused_computation.4 | custom fusion | bytes 3932800 | tf_op jit(solution)/shard_map/scatter | solution.py:90
  489.1 0.9 copy-done.2
  (33 shorter events, 0.7 us)
Async XLA Ops:
  7.2 62.0 %copy-start = (s32[2048]{0:T(1024)S(1)}, s32[2048]{0:T(1024)}, u32[]{:S(2)}) copy-start(s32[2048]{0:T(1024)} %param.7) | copy-start | bytes 24580
  7.2 36.8 %all-gather.8.cloned.1.call-start = ((), (), s32[]{:S(2)}) async-start(), calls=%async_computation.8 | async-start | bytes 1310720 | tf_op jit(solution)/shard_map/all_gather | solution.py:23
  7.9 96.3 %all-gather.10.cloned.1.call-start = ((), (), s32[]{:S(2)}) async-start(), calls=%async_computation.9 | async-start | bytes 5242880 | tf_op jit(solution)/shard_map/all_gather | solution.py:23
  61.5 23.6 %all-to-all-start = ((bf16[2,16,10,8,128]{4,3,0,2,1:T(8,128)(2,1)}), bf16[2,16,10,8,128]{4,3,0,2,1:T(8,128)(2,1)S(1)}, u32[]{:S(2)}, u32[]{:S(2)}) async-start(bf16[2,16,10,8,128]{4,3,0,2,1:T(8,128)(2,1)} %select_bitcast_fusion), calls=%async_computation | async-start | bytes 1310720 | tf_op jit(solution)/shard_map/all_to_all | solution.py:115
  68.1 149.8 %all-gather.6.cloned.1.call-start = ((), (), s32[]{:S(2)}) async-start(), calls=%async_computation.5 | async-start | bytes 8912896 | tf_op jit(solution)/shard_map/all_gather | solution.py:117
  69.1 23.9 %copy-start.3 = (bf16[512,512]{1,0:T(8,128)(2,1)S(1)}, bf16[512,512]{1,0:T(8,128)(2,1)}, u32[]{:S(2)}) copy-start(bf16[512,512]{1,0:T(8,128)(2,1)} %param.5) | copy-start | bytes 1572868
  92.0 0.8 copy-start.1
  92.9 206.1 %reduce-scatter.6.cloned.1.call-start = ((), (), s32[]{:S(2)}) async-start(), calls=%async_computation.6 | async-start | bytes 5242880 | tf_op jit(solution)/shard_map/reduce_scatter | solution.py:39
  250.8 189.8 %reduce-scatter.10.cloned.1.call-start = ((), (), s32[]{:S(2)}) async-start(), calls=%async_computation.10 | async-start | bytes 8912896
  298.6 190.4 %reduce-scatter.8.cloned.1.call-start = ((), (), s32[]{:S(2)}) async-start(), calls=%async_computation.7 | async-start | bytes 1310720 | tf_op jit(solution)/shard_map/reduce_scatter | solution.py:39
  444.0 38.0 %all-to-all-start.1 = ((bf16[2,16,10,8,128]{4,3,0,2,1:T(8,128)(2,1)}), bf16[2,16,10,8,128]{4,3,0,2,1:T(8,128)(2,1)S(1)}, u32[]{:S(2)}, u32[]{:S(2)}) async-start(bf16[2,16,10,8,128]{4,3,0,2,1:T(8,128)(2,1)} %fusion.20), calls=%async_computation.3 | async-start | bytes 1310720 | tf_op jit(solution)/shard_map/all_to_all | solution.py:155
  489.0 1.0 copy-start.2
Sparse Core Ops, SparseCore 0:
  9.8 34.1 all-gather.7
  45.8 58.3 all-gather.9
  107.3 110.5 all-gather.5
  250.9 47.2 reduce-scatter.5
  302.7 137.9 reduce-scatter.9
  443.6 38.5 reduce-scatter.7
where the time goes:
time: 498 us; the launch traced here: 497 us
  waiting for transfers between devices  342 us (69%)
  local copies, waits for them, and re-layouts  89.4 us (18%)
  matrix products  28.3 us (6%)
  between operations  14.4 us (3%)
  starting transfers between devices  13.9 us (3%)
  other arithmetic  9.23 us (2%)
    unnamed x7, waiting for transfers between devices  142 us
    all_gather x1, waiting for transfers between devices, local(): weight_block = lax.all_gather(partial_tiles, 'dp', axis=2, tiled=True)  108 us
    all_gather x2, waiting for transfers between devices, all_blocks(): tiles = lax.all_gather(tiles, axes[k])  46.9 us
    unnamed x17, local copies, waits for them, and re-layouts  41.8 us
    all_to_all x1, waiting for transfers between devices, local(): lax.all_to_all(outgoing_grads.astype(jnp.bfloat16), TP, split_axis=1, con...  30 us
    all_to_all x1, waiting for transfers between devices, local(): lax.all_to_all(outgoing, TP, split_axis=1, concat_axis=1, tiled=True)  14.5 us
    scatter x2, local copies, waits for them, and re-layouts, place_tiles(): return empty.at[:, places.reshape(-1)].set(flat, mode='drop')  13.7 us
    convert_element_type x1, local copies, waits for them, and re-layouts, local(): partial_value = jnp.einsum('nri,nmcj->mrcij', tiled_in, grads_in, preferr...  12.1 us
  transfers between devices with their start and end apart: 8, of which 6 were waited for; matrix products, arithmetic and copies ran while one was open for 19% of the time, Pallas kernels for 0%

commit v1 on v0

--- a/solution.py
+++ b/solution.py
@@ -9,6 +9,12 @@
 TILE = 128
 TP = ("tp_0", "tp_1")
 DP_TP = ("dp", "tp_0", "tp_1")
+
+
+def trade_parts(shard, mesh_axis, split, join):
+    pieces = jnp.split(shard, lax.axis_size(mesh_axis), axis=split)
+    received = lax.all_to_all(jnp.stack(pieces), mesh_axis, 0, 0)
+    return jnp.concatenate(received, axis=join)
 
 
 def joined_along(tiles, dim):
@@ -152,9 +158,9 @@
         jnp.float32
     )
     outgoing_grads = pick_tiles(summed, in_places, in_present)
-    returned = lax.all_to_all(
-        outgoing_grads.astype(jnp.bfloat16), TP, split_axis=1, concat_axis=1, tiled=True
-    ).astype(outgoing_grads.dtype)
+    returned = trade_parts(outgoing_grads.astype(jnp.bfloat16), TP, 1, 1).astype(
+        outgoing_grads.dtype
+    )
     result = place_tiles(returned, out_places, owned_count)
     return (hidden, d_normed, result)
 

time: 498 us -> 503 us (1.010)
  local copies, waits for them, and re-layouts: 89.4 us -> 99.3 us
    unnamed x17 -> x32, local copies, waits for them, and re-layouts: 41.8 us -> 51.1 us
  transfers between devices with their start and end apart: 8 -> 8, of which waited for: 6 -> 6; matrix products, arithmetic and copies ran while one was open for 19% -> 20% of each run, Pallas kernels for 0% -> 0%
where the time goes in v1:
time: 503 us; the launch traced here: 502 us
  waiting for transfers between devices  337 us (67%)
  local copies, waits for them, and re-layouts  99.3 us (20%)
  matrix products  28.3 us (6%)
  between operations  14.5 us (3%)
  starting transfers between devices  13.9 us (3%)
  other arithmetic  8.39 us (2%)
    unnamed x7, waiting for transfers between devices  142 us
    all_gather x1, waiting for transfers between devices, local(): weight_block = lax.all_gather(partial_tiles, 'dp', axis=2, tiled=True)  108 us
    unnamed x32, local copies, waits for them, and re-layouts  51.1 us
    all_gather x2, waiting for transfers between devices, all_blocks(): tiles = lax.all_gather(tiles, axes[k])  46.9 us
    all_to_all x1, waiting for transfers between devices, trade_parts(): received = lax.all_to_all(jnp.stack(pieces), mesh_axis, 0, 0)  25.6 us
    all_to_all x1, waiting for transfers between devices, local(): lax.all_to_all(outgoing, TP, split_axis=1, concat_axis=1, tiled=True)  14.5 us
    scatter x2, local copies, waits for them, and re-layouts, place_tiles(): return empty.at[:, places.reshape(-1)].set(flat, mode='drop')  13.7 us
    convert_element_type x1, local copies, waits for them, and re-layouts, local(): partial_value = jnp.einsum('nri,nmcj->mrcij', tiled_in, grads_in, preferr...  12.1 us
  transfers between devices with their start and end apart: 8, of which 6 were waited for; matrix products, arithmetic and copies ran while one was open for 20% of the time, Pallas kernels for 0%

profile of v1, /device:TPU:64, one launch (start us, length us, event | category | flops | bytes accessed | tf_op | source)
XLA Modules:
  0.0 501.5 jit_solution(18203628336199092500)
XLA Ops:
  7.2 0.7 all-gather.8.cloned.1.call-update
  8.0 36.1 %all-gather.8.cloned.1.call-done = bf16[128,4096]{1,0:T(8,128)(2,1)} async-done(((bf16[32,4096]{1,0:T(8,128)(2,1)}), bf16[128,4096]{1,0:T(8,128)(2,1)}) %all-gather.8.cloned.1.call-update) | async-done | bytes 1048592 | tf_op jit(solution)/shard_map/all_gather | solution.py:29
  44.0 0.7 add_select_fusion
  44.9 2.8 select_reduce_fusion
  47.7 0.7 compare_select_fusion.3
  48.5 0.7 multiply_reduce_fusion
  49.2 0.7 and_reduce_fusion
  49.9 8.1 %scatter_custom_fusion.2 = s32[2560]{0:T(1024)S(1)} fusion(s32[2048]{0:T(1024)S(1)} %select_bitcast_fusion.1, s32[2048]{0:T(1024)S(1)} %iota_bitcast_fusion, s32[]{:T(128)} %constant.88.clone.1), kind=kCustom, calls=%fused_computation.112 | custom fusion | bytes 10244
  58.4 1.1 constant_dynamic-slice_fusion
  59.6 0.8 gather_fusion.1
  60.4 1.1 select_bitcast_fusion
  61.5 6.7 %all-to-all-start = ((bf16[2,16,10,8,128]{4,3,0,2,1:T(8,128)(2,1)}), bf16[2,16,10,8,128]{4,3,0,2,1:T(8,128)(2,1)S(1)}, u32[]{:S(2)}, u32[]{:S(2)}) async-start(bf16[2,16,10,8,128]{4,3,0,2,1:T(8,128)(2,1)} %select_bitcast_fusion), calls=%async_computation | async-start | bytes 1310720 | tf_op jit(solution)/shard_map/all_to_all | solution.py:121
  68.3 0.2 copy.109
  68.6 0.3 bitcast_reduce_fusion
  69.1 1.4 gather_fusion
  70.6 14.5 %all-to-all-done = bf16[2,16,10,8,128]{4,3,0,2,1:T(8,128)(2,1)S(1)} async-done(((bf16[2,16,10,8,128]{4,3,0,2,1:T(8,128)(2,1)}), bf16[2,16,10,8,128]{4,3,0,2,1:T(8,128)(2,1)S(1)}, u32[]{:S(2)}, u32[]{:S(2)}) %all-to-all-start) | async-done | bytes 655392 | tf_op jit(solution)/shard_map/all_to_all | solution.py:121
  85.2 6.9 %scatter_fusion = bf16[2,128,8,128]{3,2,1,0:T(8,128)(2,1)S(1)} fusion(bf16[2,128,8,128]{3,2,1,0:T(8,128)(2,1)S(1)} %broadcast_in_dim.63, s32[160]{0:T(256)S(1)} %bitcast.228, bf16[160,2,8,128]{3,2,1,0:T(8,128)(2,1)S(1)} %bitcast.216), kind=kCustom, calls=%fused_computation.3 | custom fusion | bytes 1966720 | tf_op jit(solution)/shard_map/scatter | solution.py:96
  92.0 0.8 copy-done.1
  92.9 0.2 reduce-scatter.6.cloned.1.call-start
  93.1 0.2 copy.116
  93.3 10.9 %all-gather.10.cloned.1.call-done = bf16[16,32,4096]{2,1,0:T(8,128)(2,1)} async-done(((bf16[4,32,4096]{2,1,0:T(8,128)(2,1)}), bf16[16,32,4096]{2,1,0:T(8,128)(2,1)}) %all-gather.10.cloned.1.call-update) | async-done | bytes 4194320 | tf_op jit(solution)/shard_map/all_gather | solution.py:29
  104.2 2.5 copy.113
  106.6 3.2 copy.149
  109.9 108.0 %all-gather.6.cloned.1.call-done = bf16[2,128,128,128]{3,2,1,0:T(8,128)(2,1)} async-done(((bf16[2,128,8,128]{3,2,1,0:T(8,128)(2,1)}), bf16[2,128,128,128]{3,2,1,0:T(8,128)(2,1)}) %all-gather.6.cloned.1.call-update) | async-done | bytes 8388624 | tf_op jit(solution)/shard_map/all_gather | solution.py:123
  217.9 10.5 %fusion.4 = f32[512,2,4,128]{0,3,2,1:T(8,128)S(1)} fusion(bf16[2,32,4,128,128]{4,3,2,1,0:T(8,128)(2,1)} %bitcast.208, bf16[512,32,128,1,1]{2,1,0,4,3:T(8,128)(2,1)} %bitcast.213), kind=kOutput, calls=%fused_computation.13 | convolution fusion | flops 4294967296 | bytes 14680064 | tf_op jit(solution)/shard_map/nri,mrcij->nmcj/dot_general | solution.py:128
  228.4 0.2 fusion.53
  228.6 10.3 %copy.119 = bf16[32,128,4,128,2]{3,1,0,4,2:T(8,128)(2,1)} copy(bf16[32,128,4,128,2]{3,1,2,0,4:T(8,128)(2,1)} %bitcast.209) | data formatting | bytes 16777216 | tf_op jit(solution)/shard_map/nmcj,mrcij->nri/dot_general | solution.py:142
  238.9 0.7 fusion.8
  239.6 0.3 copy.118
  239.9 0.3 copy.117
  240.2 8.2 %bitcast_convert_fusion = bf16[512,4096]{1,0:T(8,128)(2,1)S(1)} fusion(bf16[4096,4,128,2]{2,0,3,1:T(8,128)(2,1)} %bitcast.210, bf16[512,1,4,128]{3,0,1,2:T(8,128)(2,1)S(1)} %copy.118, bf16[512,1,4,128]{3,0,1,2:T(8,128)(2,1)S(1)} %copy.117), kind=kOutput, calls=%fused_computation.7 | convolution fusion | flops 4297588736 | bytes 13631488 | tf_op jit(solution)/shard_map/nmcj,mrcij->nri/dot_general | solution.py:142
  248.3 2.5 copy.120
  250.9 9.6 %convert_bitcast_fusion = bf16[2,32,4,128,128]{3,4,1,2,0:T(8,128)(2,1)} fusion(bf16[512,32,128,1,1]{2,1,0,4,3:T(8,128)(2,1)} %bitcast.214, bf16[512,1,4,128]{3,0,1,2:T(8,128)(2,1)S(1)} %copy.118, bf16[512,1,4,128]{3,0,1,2:T(8,128)(2,1)S(1)} %copy.117), kind=kOutput, calls=%fused_computation.8 | convolution fusion | flops 4299685888 | bytes 13631488 | tf_op jit(solution)/shard_map/nri,nmcj->mrcij/dot_general | solution.py:153
  260.5 12.1 %copy.125 = bf16[2,32,4,128,128]{4,3,2,1,0:T(8,128)(2,1)} copy(bf16[2,32,4,128,128]{3,4,1,2,0:T(8,128)(2,1)} %convert_bitcast_fusion) | data formatting | bytes 16777216 | tf_op jit(solution)/shard_map/convert_element_type | solution.py:155
  272.6 12.1 %copy.147 = bf16[2,128,128,128]{3,1,0,2:T(8,128)(2,1)} copy(bf16[2,128,128,128]{3,2,1,0:T(8,128)(2,1)} %bitcast.204) | data formatting | bytes 16777216
  284.7 13.9 %copy.165 = bf16[16,8,256,128]{3,1,2,0:T(8,128)(2,1)} copy(bf16[16,8,256,128]{3,2,1,0:T(8,128)(2,1)} %bitcast.205) | data formatting | bytes 16777216
  298.8 0.1 copy.131
  299.3 141.4 %reduce-scatter.10.cloned.1.call-done = bf16[8,32768]{1,0:T(8,128)(2,1)} async-done(((bf16[128,32768]{1,0:T(8,128)(2,1)}), bf16[8,32768]{1,0:T(8,128)(2,1)}) %reduce-scatter.10.cloned.1.call-update) | async-done | bytes 524304
  440.7 1.1 copy.151
  441.8 0.3 copy.164
  442.1 0.8 gather_fusion.2
  442.9 0.2 fusion.20
  443.2 0.6 fusion.37
  443.8 0.6 fusion.36
  444.4 0.6 fusion.35
  445.0 0.6 fusion.34
  445.7 0.6 fusion.33
  446.3 0.6 fusion.32
  446.9 0.6 fusion.31
  447.5 0.6 fusion.30
  448.1 0.6 fusion.29
  448.8 0.6 fusion.28
  449.4 0.6 fusion.27
  450.0 0.6 fusion.26
  450.6 0.6 fusion.25
  451.2 0.6 fusion.24
  451.9 0.6 fusion.23
  452.5 0.6 fusion.22
  453.1 6.8 %all-to-all-start.1 = ((bf16[16,2,1,10,8,128]{5,4,1,3,2,0:T(8,128)(2,1)}), bf16[16,2,1,10,8,128]{5,4,1,3,2,0:T(8,128)(2,1)S(1)}, u32[]{:S(2)}, u32[]{:S(2)}) async-start(bf16[16,2,1,10,8,128]{5,4,1,3,2,0:T(8,128)(2,1)} %fusion.22), calls=%async_computation.3 | async-start | bytes 1310720 | tf_op jit(solution)/shard_map/all_to_all | solution.py:16
  460.1 1.0 copy.133
  461.1 25.6 %all-to-all-done.1 = bf16[16,2,1,10,8,128]{5,4,1,3,2,0:T(8,128)(2,1)S(1)} async-done(((bf16[16,2,1,10,8,128]{5,4,1,3,2,0:T(8,128)(2,1)}), bf16[16,2,1,10,8,128]{5,4,1,3,2,0:T(8,128)(2,1)S(1)}, u32[]{:S(2)}, u32[]{:S(2)}) %all-to-all-start.1) | async-done | bytes 655392 | tf_op jit(solution)/shard_map/all_to_all | solution.py:16
  486.7 0.1 convert_element_type.56
  486.9 6.8 %scatter_fusion.1 = f32[2,128,8,128]{3,2,1,0:T(8,128)S(1)} fusion(f32[2,128,8,128]{3,2,1,0:T(8,128)S(1)} %broadcast_in_dim.71, s32[160]{0:T(256)S(1)} %bitcast.229, f32[160,2,8,128]{3,2,1,0:T(8,128)S(1)} %bitcast.211), kind=kCustom, calls=%fused_computation.4 | custom fusion | bytes 3932800 | tf_op jit(solution)/shard_map/scatter | solution.py:96
  493.8 0.9 copy-done.2
  (49 shorter events, 2.0 us)
Async XLA Ops:
  7.2 62.0 %copy-start = (s32[2048]{0:T(1024)S(1)}, s32[2048]{0:T(1024)}, u32[]{:S(2)}) copy-start(s32[2048]{0:T(1024)} %param.7) | copy-start | bytes 24580
  7.2 36.8 %all-gather.8.cloned.1.call-start = ((), (), s32[]{:S(2)}) async-start(), calls=%async_computation.8 | async-start | bytes 1310720 | tf_op jit(solution)/shard_map/all_gather | solution.py:29
  7.9 96.3 %all-gather.10.cloned.1.call-start = ((), (), s32[]{:S(2)}) async-start(), calls=%async_computation.9 | async-start | bytes 5242880 | tf_op jit(solution)/shard_map/all_gather | solution.py:29
  61.5 23.6 %all-to-all-start = ((bf16[2,16,10,8,128]{4,3,0,2,1:T(8,128)(2,1)}), bf16[2,16,10,8,128]{4,3,0,2,1:T(8,128)(2,1)S(1)}, u32[]{:S(2)}, u32[]{:S(2)}) async-start(bf16[2,16,10,8,128]{4,3,0,2,1:T(8,128)(2,1)} %select_bitcast_fusion), calls=%async_computation | async-start | bytes 1310720 | tf_op jit(solution)/shard_map/all_to_all | solution.py:121
  68.1 149.8 %all-gather.6.cloned.1.call-start = ((), (), s32[]{:S(2)}) async-start(), calls=%async_computation.5 | async-start | bytes 8912896 | tf_op jit(solution)/shard_map/all_gather | solution.py:123
  69.1 23.9 %copy-start.3 = (bf16[512,512]{1,0:T(8,128)(2,1)S(1)}, bf16[512,512]{1,0:T(8,128)(2,1)}, u32[]{:S(2)}) copy-start(bf16[512,512]{1,0:T(8,128)(2,1)} %param.5) | copy-start | bytes 1572868
  92.0 0.8 copy-start.1
  92.9 206.4 %reduce-scatter.6.cloned.1.call-start = ((), (), s32[]{:S(2)}) async-start(), calls=%async_computation.6 | async-start | bytes 5242880 | tf_op jit(solution)/shard_map/reduce_scatter | solution.py:45
  250.8 189.8 %reduce-scatter.10.cloned.1.call-start = ((), (), s32[]{:S(2)}) async-start(), calls=%async_computation.10 | async-start | bytes 8912896
  298.6 195.1 %reduce-scatter.8.cloned.1.call-start = ((), (), s32[]{:S(2)}) async-start(), calls=%async_computation.7 | async-start | bytes 1310720 | tf_op jit(solution)/shard_map/reduce_scatter | solution.py:45
  453.1 33.6 %all-to-all-start.1 = ((bf16[16,2,1,10,8,128]{5,4,1,3,2,0:T(8,128)(2,1)}), bf16[16,2,1,10,8,128]{5,4,1,3,2,0:T(8,128)(2,1)S(1)}, u32[]{:S(2)}, u32[]{:S(2)}) async-start(bf16[16,2,1,10,8,128]{5,4,1,3,2,0:T(8,128)(2,1)} %fusion.22), calls=%async_computation.3 | async-start | bytes 1310720 | tf_op jit(solution)/shard_map/all_to_all | solution.py:16
  493.7 1.0 copy-start.2
Sparse Core Ops, SparseCore 0:
  9.8 34.1 all-gather.7
  45.8 58.3 all-gather.9
  107.3 110.5 all-gather.5
  250.9 47.2 reduce-scatter.5
  302.7 137.9 reduce-scatter.9
  443.6 39.3 reduce-scatter.7
